TPU v7x, 32 devices: a whole 2x2x4 slice. The times are simulated.
32 devices in a mesh: row: 4 (over z), col: 8 (over y, x, core).
Axes of the slice: x: 2, y: 2, z: 4, core: 2. Of those that a mesh axis runs over, the one named last changes fastest.
Arguments:
- minus_gradient: float32 [6, 16384], P(None, ('row', 'col')), may hold values from -10 to 10
- diag_blocks: float32 [36, 16384], P(None, ('row', 'col')), may hold values from -1000 to 1000, as said below
- hess_blocks: float32 [4, 8, 36, 4096], P('row', 'col'), may hold values from -40 to 40, as said below
- block_rows: int32 [4, 8, 4096], P('row', 'col'), may hold values from 0 to 2047
- block_cols: int32 [4, 8, 4096], P('row', 'col'), may hold values from 0 to 4095
- block_counts: int32 [4, 8], P('row', 'col'), may hold values from 0 to 4096, as said below
Outputs:
- pose_update: float32 [6, 16384], P(None, ('row', 'col'))
- residual: float32 [6, 16384], P(None, ('row', 'col'))
Inputs may be any that keep to these rules, and one draw needn't show every extreme that they name: `hess_blocks`: the live blocks of all tiles together with diag_blocks form a symmetric positive definite matrix; no live block lies on the diagonal; the slots after the live ones hold arbitrary entries. `diag_blocks`: each 6x6 block is symmetric positive definite. The live slots of a tile are its first block_counts slots.
All inputs are finite; a program needn't handle non-finite values.
Results may differ from a plain program's by a relative error of at most 0.0003.
Values sent between devices are 32-bit elements; how exact they have to be, the bound alone decides.
No kernel may reach another device: no remote copies, remote signals or barrier semaphores. Data moves between devices by JAX's collectives and lax.ppermute only.
A program may use at most 64 MiB of HBM per device.

v0:
```python
import math

import jax
import jax.numpy as jnp
from jax import lax
from jax.sharding import PartitionSpec as P

ITERS = 3


def factor_blocks(blocks):
    lower_part = {}
    reciprocals = []
    for j in range(6):
        pivot_value = blocks[7 * j]
        for k in range(j):
            pivot_value = pivot_value - lower_part[j, k] * lower_part[j, k]
        reciprocal = 1.0 / jnp.sqrt(pivot_value)
        reciprocals.append(reciprocal)
        for i in range(j + 1, 6):
            entry_value = blocks[6 * i + j]
            for k in range(j):
                entry_value = entry_value - lower_part[i, k] * lower_part[j, k]
            lower_part[i, j] = entry_value * reciprocal
    return (lower_part, reciprocals)


def apply_inverse(lower_part, reciprocals, vector):
    forward = []
    for i in range(6):
        running = vector[i]
        for k in range(i):
            running = running - lower_part[i, k] * forward[k]
        forward.append(running * reciprocals[i])
    backward = [None] * 6
    for i in range(5, -1, -1):
        running = forward[i]
        for k in range(i + 1, 6):
            running = running - lower_part[k, i] * backward[k]
        backward[i] = running * reciprocals[i]
    return jnp.stack(backward)


def diagonal_term(diag_blocks, vector):
    return jnp.sum(diag_blocks.reshape(6, 6, -1) * vector[None], axis=1)


def pick_columns(source, offsets):
    width = source.shape[1]
    low_width = math.gcd(128, width)
    high_width = width // low_width
    table = source.reshape(6 * high_width, low_width)
    slot_count = offsets.shape[0]
    block_size = math.gcd(512, slot_count)
    turns = slot_count // block_size

    def pick_one_block(carry, offset):
        low_part = offset % low_width
        high_part = offset // low_width
        low_onehot = (
            lax.broadcasted_iota(jnp.int32, (low_width, block_size), 0) == low_part[None, :]
        ).astype(jnp.float32)
        spread = jnp.dot(
            table, low_onehot, precision=lax.Precision.HIGHEST, preferred_element_type=jnp.float32
        )
        high_onehot = (
            lax.broadcasted_iota(jnp.int32, (high_width, block_size), 0) == high_part[None, :]
        ).astype(jnp.float32)
        chosen = jnp.sum(spread.reshape(6, high_width, block_size) * high_onehot[None], axis=1)
        return (carry, chosen)

    unused, blocks_out = lax.scan(pick_one_block, None, offsets.reshape(turns, block_size))
    return jnp.transpose(blocks_out, (1, 0, 2)).reshape(6, slot_count)


def add_rows(terms, rows, span_size):
    low_width = math.gcd(128, span_size)
    high_width = span_size // low_width
    slot_count = rows.shape[0]
    block_size = math.gcd(512, slot_count)
    turns = slot_count // block_size
    term_blocks = jnp.transpose(terms.reshape(6, turns, block_size), (1, 0, 2))
    row_blocks = rows.reshape(turns, block_size)

    def add_one_block(carry, inputs):
        term_block, row_block = inputs
        high_onehot = (
            lax.broadcasted_iota(jnp.int32, (high_width, block_size), 0)
            == (row_block // low_width)[None, :]
        ).astype(jnp.float32)
        spread = (term_block[:, None, :] * high_onehot[None]).reshape(6 * high_width, block_size)
        low_onehot = (
            (row_block % low_width)[:, None]
            == lax.broadcasted_iota(jnp.int32, (block_size, low_width), 1)
        ).astype(jnp.float32)
        carry = carry + jnp.dot(
            spread, low_onehot, precision=lax.Precision.HIGHEST, preferred_element_type=jnp.float32
        )
        return (carry, None)

    start_total = jnp.zeros((6 * high_width, low_width), jnp.float32)
    total, unused = lax.scan(add_one_block, start_total, (term_blocks, row_blocks))
    return total.reshape(6, span_size)


def merged_sums(residual, precond, hess_image):
    return lax.psum((jnp.sum(residual * precond), jnp.sum(hess_image * precond)), ("row", "col"))


def on_device(minus_gradient, diag_blocks, hess_blocks, block_rows, block_cols, block_counts):
    pose_dev = minus_gradient.shape[1]
    blocks = hess_blocks.reshape(6, 6, -1)
    local_rows = block_rows.reshape(-1)
    local_cols = block_cols.reshape(-1)
    slot_count = local_rows.shape[0]
    live_mask = jnp.arange(slot_count, dtype=jnp.int32) < block_counts.reshape(())
    span_size = pose_dev * lax.axis_size("row")
    lower_part, reciprocals = factor_blocks(diag_blocks)

    def tile_terms(picked):
        return jnp.sum(blocks * picked[None], axis=1)

    def hessian(vector):
        gathered = lax.all_gather(vector, "col", axis=1, tiled=True)
        picked = pick_columns(gathered, local_cols)
        live_terms = jnp.where(live_mask[None, :], tile_terms(picked), 0.0)
        partial_value = add_rows(live_terms, local_rows, span_size)
        own_term = diagonal_term(diag_blocks, vector)
        summed = lax.psum(partial_value, "row")
        reduced = lax.dynamic_slice_in_dim(summed, lax.axis_index("row") * pose_dev, pose_dev, 1)
        return reduced + own_term

    solution = jnp.zeros_like(minus_gradient)
    residual = minus_gradient
    precond = apply_inverse(lower_part, reciprocals, residual)
    hess_image = hessian(precond)
    rho_now, curv_value = merged_sums(residual, precond, hess_image)
    step_size = rho_now / curv_value
    direction = precond
    along_image = hess_image
    for k in range(ITERS):
        solution = solution + step_size * direction
        residual = residual - step_size * along_image
        if k + 1 < ITERS:
            precond = apply_inverse(lower_part, reciprocals, residual)
            hess_image = hessian(precond)
            rho_next, curv_value = merged_sums(residual, precond, hess_image)
            ratio_next = rho_next / rho_now
            step_size = rho_next / (curv_value - ratio_next * rho_next / step_size)
            direction = precond + ratio_next * direction
            along_image = hess_image + ratio_next * along_image
            rho_now = rho_next
    return (solution, residual)


def solution(mesh):
    placed = (
        P(None, ("row", "col")),
        P(None, ("row", "col")),
        P("row", "col", None, None),
        P("row", "col", None),
        P("row", "col", None),
        P("row", "col"),
    )
    return jax.shard_map(
        on_device,
        mesh=mesh,
        in_specs=placed,
        out_specs=(P(None, ("row", "col")), P(None, ("row", "col"))),
        check_vma=False,
    )
```

profile of v0, /device:TPU:0, one launch (start us, length us, event | category | flops | bytes accessed | tf_op | source)
XLA Modules:
  0.0 246.5 jit_solution(5160269623161957242)
XLA Ops:
  0.6 1.1 subtract_multiply_fusion.21
  1.7 0.7 copy-done.2
  2.6 10.7 %all_gather.9 = f32[6,4096]{1,0:T(8,128)S(1)} all-gather(f32[6,512]{1,0:T(8,128)S(1)} %stack.6), channel_id=1, replica_groups=mesh['row'=4,'col'=8] {'col'}, dimensions={1}, use_global_device_ids=true | all-gather | bytes 110592 | tf_op jit(solution)/shard_map/all_gather | solution.py:124
  14.0 0.7 reduce.7
  14.7 3.9 %while.75 = (s32[]{:T(128)}, f32[8,6,512]{2,1,0:T(8,128)S(1)}, s32[8,512]{1,0:T(8,128)S(1)}, f32[192,128]{1,0:T(8,128)S(1)}, s32[]{:T(128)}) while((s32[]{:T(128)}, f32[8,6,512]{2,1,0:T(8,128)S(1)}, s32[8,512]{1,0:T(8,128)S(1)}, f32[192,128]{1,0:T(8,128)S(1)}, s32[]{:T(128)}) %tuple.218), condition=%wide.region_4.5_spmd, body=%wide.region_2.4_spmd.sunk | while | flops 151297024 | bytes 1075269 | solution.py:72
  18.7 1.4 reduce
  21.1 0.7 copy-done.4
  21.8 0.7 reduce.8
  22.5 3.9 %while.78 = (s32[]{:T(128)}, f32[96,128]{1,0:T(8,128)S(1)}, f32[8,6,512]{2,1,0:T(8,128)S(1)}, s32[8,512]{1,0:T(8,128)S(1)}, s32[]{:T(128)}, /*index=5*/s32[]{:T(128)}) while((s32[]{:T(128)}, f32[96,128]{1,0:T(8,128)S(1)}, f32[8,6,512]{2,1,0:T(8,128)S(1)}, s32[8,512]{1,0:T(8,128)S(1)}, s32[]{:T(128)}, /*index=5*/s32[]{:T(128)}) %tuple.221), condition=%wide.region_7.8_spmd.clone, body=%wide.region_6.7_spmd.clone.sunk | while | flops 75666432 | bytes 608343 | solution.py:102
  26.4 19.9 %psum.64 = f32[6,2048]{1,0:T(8,128)S(1)} all-reduce(f32[6,2048]{1,0:T(8,128)S(1)} %reshape.316), channel_id=1, replica_groups=mesh['row'=4,'col'=8] {'row'}, use_global_device_ids=true, to_apply=%region_8.9 | all-reduce | flops 12288 | bytes 98304 | tf_op jit(solution)/shard_map/psum | solution.py:129
  47.0 37.8 %all-reduce.2 = (f32[]{:T(128)}, f32[]{:T(128)}) all-reduce(f32[]{:T(128)} %get-tuple-element.394, f32[]{:T(128)} %get-tuple-element.393), channel_id=1, replica_groups=mesh['row'=4,'col'=8] {'row','col'}, use_global_device_ids=true, to_apply=%region_1.2 | all-reduce | flops 2 | bytes 16 | tf_op jit(solution)/shard_map/psum | solution.py:107
  86.3 10.2 %all_gather.10 = f32[6,4096]{1,0:T(8,128)S(1)} all-gather(f32[6,512]{1,0:T(8,128)S(1)} %stack.7), channel_id=1, replica_groups=mesh['row'=4,'col'=8] {'col'}, dimensions={1}, use_global_device_ids=true | all-gather | bytes 110592 | tf_op jit(solution)/shard_map/all_gather | solution.py:124
  96.5 3.9 %while.76 = (s32[]{:T(128)}, f32[8,6,512]{2,1,0:T(8,128)S(1)}, s32[8,512]{1,0:T(8,128)S(1)}, f32[192,128]{1,0:T(8,128)S(1)}, s32[]{:T(128)}) while((s32[]{:T(128)}, f32[8,6,512]{2,1,0:T(8,128)S(1)}, s32[8,512]{1,0:T(8,128)S(1)}, f32[192,128]{1,0:T(8,128)S(1)}, s32[]{:T(128)}) %tuple.236), condition=%wide.region_16.17_spmd, body=%wide.region_14.16_spmd.sunk | while | flops 151297024 | bytes 1075269 | solution.py:72
  100.8 3.9 %while.79 = (s32[]{:T(128)}, f32[96,128]{1,0:T(8,128)S(1)}, f32[8,6,512]{2,1,0:T(8,128)S(1)}, s32[8,512]{1,0:T(8,128)S(1)}, s32[]{:T(128)}, /*index=5*/s32[]{:T(128)}) while((s32[]{:T(128)}, f32[96,128]{1,0:T(8,128)S(1)}, f32[8,6,512]{2,1,0:T(8,128)S(1)}, s32[8,512]{1,0:T(8,128)S(1)}, s32[]{:T(128)}, ...), condition=%wide.region_19.20_spmd.clone, body=%wide.region_18.19_spmd.clone.sunk | while | flops 75666432 | bytes 608343 | solution.py:102
  104.7 18.5 %psum.67 = f32[6,2048]{1,0:T(8,128)S(1)} all-reduce(f32[6,2048]{1,0:T(8,128)S(1)} %reshape.319), channel_id=1, replica_groups=mesh['row'=4,'col'=8] {'row'}, use_global_device_ids=true, to_apply=%region_20.21 | all-reduce | flops 12288 | bytes 98304 | tf_op jit(solution)/shard_map/psum | solution.py:129
  123.2 0.7 multiply_reduce_fusion.11
  123.9 37.8 %all-reduce.1 = (f32[]{:T(128)}, f32[]{:T(128)}) all-reduce(f32[]{:T(128)} %get-tuple-element.392, f32[]{:T(128)} %get-tuple-element.391), channel_id=1, replica_groups=mesh['row'=4,'col'=8] {'row','col'}, use_global_device_ids=true, to_apply=%region_13.14 | all-reduce | flops 2 | bytes 16 | tf_op jit(solution)/shard_map/psum | solution.py:107
  166.4 10.2 %all_gather.11 = f32[6,4096]{1,0:T(8,128)S(1)} all-gather(f32[6,512]{1,0:T(8,128)S(1)} %stack.8), channel_id=1, replica_groups=mesh['row'=4,'col'=8] {'col'}, dimensions={1}, use_global_device_ids=true | all-gather | bytes 110592 | tf_op jit(solution)/shard_map/all_gather | solution.py:124
  176.7 3.9 %while.77 = (s32[]{:T(128)}, f32[8,6,512]{2,1,0:T(8,128)S(1)}, s32[8,512]{1,0:T(8,128)S(1)}, f32[192,128]{1,0:T(8,128)S(1)}, s32[]{:T(128)}) while((s32[]{:T(128)}, f32[8,6,512]{2,1,0:T(8,128)S(1)}, s32[8,512]{1,0:T(8,128)S(1)}, f32[192,128]{1,0:T(8,128)S(1)}, s32[]{:T(128)}) %tuple.237), condition=%wide.region_28.29_spmd, body=%wide.region_26.28_spmd.sunk | while | flops 151297024 | bytes 1075269 | solution.py:72
  181.0 3.9 %while.80 = (s32[]{:T(128)}, f32[96,128]{1,0:T(8,128)S(1)}, f32[8,6,512]{2,1,0:T(8,128)S(1)}, s32[8,512]{1,0:T(8,128)S(1)}, s32[]{:T(128)}, /*index=5*/s32[]{:T(128)}) while((s32[]{:T(128)}, f32[96,128]{1,0:T(8,128)S(1)}, f32[8,6,512]{2,1,0:T(8,128)S(1)}, s32[8,512]{1,0:T(8,128)S(1)}, s32[]{:T(128)}, ...), condition=%wide.region_31.32_spmd.clone, body=%wide.region_30.31_spmd.clone.sunk | while | flops 75666432 | bytes 608343 | solution.py:102
  184.9 18.7 %psum.70 = f32[6,2048]{1,0:T(8,128)S(1)} all-reduce(f32[6,2048]{1,0:T(8,128)S(1)} %reshape.321), channel_id=1, replica_groups=mesh['row'=4,'col'=8] {'row'}, use_global_device_ids=true, to_apply=%region_32.33 | all-reduce | flops 12288 | bytes 98304 | tf_op jit(solution)/shard_map/psum | solution.py:129
  203.6 0.6 multiply_reduce_fusion.9
  204.2 37.7 %all-reduce = (f32[]{:T(128)}, f32[]{:T(128)}) all-reduce(f32[]{:T(128)} %get-tuple-element.390, f32[]{:T(128)} %get-tuple-element.389), channel_id=1, replica_groups=mesh['row'=4,'col'=8] {'row','col'}, use_global_device_ids=true, to_apply=%region_25.26 | all-reduce | flops 2 | bytes 16 | tf_op jit(solution)/shard_map/psum | solution.py:107
  245.9 0.6 multiply_subtract_fusion
  (334 shorter events, 23.5 us)
Async XLA Ops:
  0.6 1.1 copy-start.1
  1.7 0.7 copy-start.2
  13.3 0.7 copy-start.3
  14.7 4.0 %copy-start = (f32[1,1,36,4096]{3,1,2,0:T(1,128)S(1)}, f32[1,1,36,4096]{3,1,2,0:T(1,128)}, u32[]{:S(2)}) copy-start(f32[1,1,36,4096]{3,1,2,0:T(1,128)} %param.20) | copy-start | bytes 1769476
  21.1 0.7 copy-start.4
where the time goes:
time: 248 us; the launch traced here: 247 us
  blocking collectives  201 us (81%)
  matrix products  16.6 us (7%)
  between operations  11.5 us (5%)
  other arithmetic  11.1 us (4%)
  loops' own time  2.93 us (1%)
  local copies, waits for them, and re-layouts  2.92 us (1%)
    psum x3, blocking collectives, merged_sums(): lax.psum((jnp.sum(residual * precond), jnp.sum(hess_image * precond)), ('...  113 us
    psum x3, blocking collectives, hessian(): summed = lax.psum(partial_value, 'row')  57.1 us
    all_gather x3, blocking collectives, hessian(): gathered = lax.all_gather(vector, 'col', axis=1, tiled=True)  31.1 us
    dot_general x24, matrix products, add_one_block(): jnp.dot(spread, low_onehot, precision=lax.Precision.HIGHEST, preferred_el...  8.61 us
    dot_general x24, matrix products, pick_one_block(): jnp.dot(table, low_onehot, precision=lax.Precision.HIGHEST, preferred_ele...  7.99 us

commit v1 on v0

v1 whole, which is shorter than its diff:
```python
import jax
import jax.numpy as jnp
from jax import lax
from jax.experimental import pallas as pl
from jax.experimental.pallas import tpu as pltpu
from jax.sharding import PartitionSpec as P

ITERS = 3
LANES = 128


def factor_blocks(blocks):
    lower_part = {}
    reciprocals = []
    for j in range(6):
        pivot_value = blocks[7 * j]
        for k in range(j):
            pivot_value = pivot_value - lower_part[j, k] * lower_part[j, k]
        reciprocal = 1.0 / jnp.sqrt(pivot_value)
        reciprocals.append(reciprocal)
        for i in range(j + 1, 6):
            entry_value = blocks[6 * i + j]
            for k in range(j):
                entry_value = entry_value - lower_part[i, k] * lower_part[j, k]
            lower_part[i, j] = entry_value * reciprocal
    return (lower_part, reciprocals)


def apply_inverse(lower_part, reciprocals, vector):
    forward = []
    for i in range(6):
        running = vector[i]
        for k in range(i):
            running = running - lower_part[i, k] * forward[k]
        forward.append(running * reciprocals[i])
    backward = [None] * 6
    for i in range(5, -1, -1):
        running = forward[i]
        for k in range(i + 1, 6):
            running = running - lower_part[k, i] * backward[k]
        backward[i] = running * reciprocals[i]
    return backward


def split_three(value):
    high = value.astype(jnp.bfloat16)
    rest = value - high.astype(jnp.float32)
    middle = rest.astype(jnp.bfloat16)
    low = (rest - middle.astype(jnp.float32)).astype(jnp.bfloat16)
    return high, middle, low


def exact_dot(left, onehot, dims):
    parts = [
        lax.dot_general(piece, onehot, (dims, ((), ())), preferred_element_type=jnp.float32)
        for piece in split_three(left)
    ]
    return parts[2] + parts[1] + parts[0]


def tile_kernel(count_ref, table_ref, cols_ref, rows_ref, blocks_ref, out_ref, *, chunk):
    high_in = table_ref.shape[0] // 6
    high_out = out_ref.shape[0] // 6
    slots = cols_ref.shape[1]
    live = count_ref[0, 0]
    table = table_ref[...]
    out_ref[...] = jnp.zeros_like(out_ref)

    def one_chunk(start):
        cols = cols_ref[:, pl.ds(start, chunk)]
        rows = rows_ref[:, pl.ds(start, chunk)]
        lane_ids = lax.broadcasted_iota(jnp.int32, (LANES, chunk), 0)
        low_in = jnp.where(lane_ids == cols % LANES, 1.0, 0.0).astype(jnp.bfloat16)
        spread = exact_dot(table, low_in, ((1,), (0,)))
        pick = lax.broadcasted_iota(jnp.int32, (high_in, chunk), 0) == cols // LANES
        picked = [
            jnp.sum(
                jnp.where(pick, spread[b * high_in : (b + 1) * high_in], 0.0),
                axis=0,
                keepdims=True,
            )
            for b in range(6)
        ]
        is_live = lax.broadcasted_iota(jnp.int32, (1, chunk), 1) + start < live
        place = lax.broadcasted_iota(jnp.int32, (high_out, chunk), 0) == rows // LANES
        terms = []
        for a in range(6):
            term = blocks_ref[6 * a : 6 * a + 1, pl.ds(start, chunk)] * picked[0]
            for b in range(1, 6):
                entry = blocks_ref[6 * a + b : 6 * a + b + 1, pl.ds(start, chunk)]
                term = term + entry * picked[b]
            term = jnp.where(is_live, term, 0.0)
            terms.append(jnp.where(place, term, 0.0))
        low_out = jnp.where(lane_ids == rows % LANES, 1.0, 0.0).astype(jnp.bfloat16)
        out_ref[...] += exact_dot(jnp.concatenate(terms, axis=0), low_out, ((1,), (1,)))

    for turn in range(slots // chunk):
        @pl.when(turn * chunk < live)
        def _():
            one_chunk(turn * chunk)


def tile_product(count, table, cols, rows, blocks, high_out):
    slots = cols.shape[1]
    chunk = min(512, slots)
    vmem = pl.BlockSpec(memory_space=pltpu.VMEM)
    return pl.pallas_call(
        lambda *refs: tile_kernel(*refs, chunk=chunk),
        out_shape=jax.ShapeDtypeStruct((6 * high_out, LANES), jnp.float32),
        in_specs=[pl.BlockSpec(memory_space=pltpu.SMEM), vmem, vmem, vmem, vmem],
        out_specs=vmem,
        name="tile_product",
    )(count, table, cols, rows, blocks)


def on_device(minus_gradient, diag_blocks, hess_blocks, block_rows, block_cols, block_counts):
    pose_dev = minus_gradient.shape[1]
    high = pose_dev // LANES
    n_row = lax.axis_size("row")
    n_col = lax.axis_size("col")
    rows_own = 6 * high
    diag = diag_blocks.reshape(36, high, LANES)
    blocks = hess_blocks.reshape(36, -1)
    rows = block_rows.reshape(1, -1)
    cols = block_cols.reshape(1, -1)
    lower_part, reciprocals = factor_blocks(diag)

    def precondition(vector):
        return jnp.stack(apply_inverse(lower_part, reciprocals, vector))

    def lane_sums(left_a, right_a, left_b, right_b):
        first = jnp.sum(left_a * right_a, axis=(0, 1))
        second = jnp.sum(left_b * right_b, axis=(0, 1))
        return jnp.stack([first, second])

    def hessian(vector, sums):
        mine = jnp.concatenate([vector.reshape(rows_own, LANES), sums], axis=0)
        sent = jnp.broadcast_to(mine[None], (n_col,) + mine.shape)
        got = lax.all_to_all(sent, "col", 0, 0)
        table = got[:, :rows_own].reshape(n_col, 6, high, LANES)
        table = jnp.transpose(table, (1, 0, 2, 3)).reshape(6 * n_col * high, LANES)
        group_sums = jnp.sum(got[:, rows_own:], axis=0)
        partial = tile_product(block_counts, table, cols, rows, blocks, n_row * high)
        partial = jnp.transpose(partial.reshape(6, n_row, high, LANES), (1, 0, 2, 3))
        partial = partial.reshape(n_row, rows_own, LANES)
        spread_sums = jnp.broadcast_to(group_sums[None], (n_row,) + group_sums.shape)
        back = lax.all_to_all(jnp.concatenate([partial, spread_sums], axis=1), "row", 0, 0)
        back = jnp.sum(back, axis=0)
        own_term = jnp.sum(diag.reshape(6, 6, high, LANES) * vector[None], axis=1)
        image = back[:rows_own].reshape(6, high, LANES) + own_term
        return image, jnp.sum(back[rows_own:], axis=1)

    def total_sums(sums):
        sent = jnp.broadcast_to(sums[None], (n_col,) + sums.shape)
        sums = jnp.sum(lax.all_to_all(sent, "col", 0, 0), axis=0)
        sent = jnp.broadcast_to(sums[None], (n_row,) + sums.shape)
        sums = jnp.sum(lax.all_to_all(sent, "row", 0, 0), axis=0)
        return jnp.sum(sums, axis=1)

    residual = minus_gradient.reshape(6, high, LANES)
    update = jnp.zeros_like(residual)
    precond = precondition(residual)
    image, unused = hessian(precond, jnp.zeros((2, LANES), jnp.float32))
    for k in range(ITERS):
        sums = lane_sums(residual, precond, image, precond)
        last = k + 1 == ITERS
        if last:
            totals = total_sums(sums)
        else:
            image_pre = precondition(image)
            image_next, totals = hessian(image_pre, sums)
        rho, curv = totals[0], totals[1]
        if k == 0:
            step = rho / curv
            direction, along = precond, image
        else:
            ratio = rho / rho_before
            step = rho / (curv - ratio * rho / step)
            direction = precond + ratio * direction
            along = image + ratio * along
        update = update + step * direction
        residual = residual - step * along
        if not last:
            if k == 0:
                along_pre, along_next = image_pre, image_next
            else:
                along_pre = image_pre + ratio * along_pre
                along_next = image_next + ratio * along_next
            precond = precond - step * along_pre
            image = image - step * along_next
        rho_before = rho
    return (update.reshape(6, pose_dev), residual.reshape(6, pose_dev))


def solution(mesh):
    vectors = P(None, ("row", "col"))
    return jax.shard_map(
        on_device,
        mesh=mesh,
        in_specs=(
            vectors,
            vectors,
            P("row", "col", None, None),
            P("row", "col", None),
            P("row", "col", None),
            P("row", "col"),
        ),
        out_specs=(vectors, vectors),
        check_vma=False,
    )
```

time: 248 us -> 113 us (0.46)
  blocking collectives: 201 us -> 7.35 us
  waiting for transfers between devices: 0 us -> 36.8 us
  starting transfers between devices: 0 us -> 27.5 us
  matrix products: 16.6 us -> 0 us
  Pallas kernels: 0 us -> 12.3 us
  local copies, waits for them, and re-layouts: 2.92 us -> 12.2 us
  other arithmetic: 11.1 us -> 3.81 us
  loops' own time: 2.93 us -> 0 us
    psum x6 -> x0, blocking collectives: 170 us -> none  [the longest x3 113 us: merged_sums(): lax.psum((jnp.sum(residual * precond), jnp.sum(hess_image * precond)), ('...]
    all_to_all x0 -> x7, waiting for transfers between devices: none -> 36.8 us  [the longest x3 17.1 us: hessian(): lax.all_to_all(jnp.concatenate([partial, spread_sums], axis=1), 'row', 0, 0)]
    all_gather x3 -> x0, blocking collectives: 31.1 us -> none  [hessian(): gathered = lax.all_gather(vector, 'col', axis=1, tiled=True)]
    all_to_all x0 -> x7, starting transfers between devices: none -> 27.5 us  [the longest x3 12.8 us: hessian(): got = lax.all_to_all(sent, 'col', 0, 0)]
    dot_general x48 -> x0, matrix products: 16.6 us -> none  [the longest x24 8.61 us: add_one_block(): jnp.dot(spread, low_onehot, precision=lax.Precision.HIGHEST, preferred_el...]
    pallas_call x0 -> x3, Pallas kernels: none -> 12.3 us  [tile_product(): pl.pallas_call(lambda *refs: tile_kernel(*refs, chunk=chunk), out_shape=j...]
    all_to_all x0 -> x1, blocking collectives: none -> 7.35 us  [total_sums(): sums = jnp.sum(lax.all_to_all(sent, 'col', 0, 0), axis=0)]
    slice x0 -> x9, local copies, waits for them, and re-layouts: none -> 3.75 us  [the longest x3 1.84 us: on_device(): rho, curv = (totals[0], totals[1])]
  transfers between devices with their start and end apart: 0 -> 7, of which waited for: 0 -> 7; matrix products, arithmetic and copies ran while one was open for 0% -> 1% of each run, Pallas kernels for 0% -> 0%
where the time goes in v1:
time: 113 us; the launch traced here: 111 us
  waiting for transfers between devices  36.8 us (33%)
  starting transfers between devices  27.5 us (24%)
  Pallas kernels  12.3 us (11%)
  local copies, waits for them, and re-layouts  12.2 us (11%)
  between operations  11.1 us (10%)
  blocking collectives  7.35 us (7%)
  other arithmetic  3.81 us (3%)
    all_to_all x3, waiting for transfers between devices, hessian(): lax.all_to_all(jnp.concatenate([partial, spread_sums], axis=1), 'row', 0, 0)  17.1 us
    all_to_all x3, waiting for transfers between devices, hessian(): got = lax.all_to_all(sent, 'col', 0, 0)  14.2 us
    all_to_all x3, starting transfers between devices, hessian(): got = lax.all_to_all(sent, 'col', 0, 0)  12.8 us
    pallas_call x3, Pallas kernels, tile_product(): pl.pallas_call(lambda *refs: tile_kernel(*refs, chunk=chunk), out_shape=j...  12.3 us
    all_to_all x3, starting transfers between devices, hessian(): lax.all_to_all(jnp.concatenate([partial, spread_sums], axis=1), 'row', 0, 0)  11.4 us
    all_to_all x1, blocking collectives, total_sums(): sums = jnp.sum(lax.all_to_all(sent, 'col', 0, 0), axis=0)  7.35 us
    all_to_all x1, waiting for transfers between devices, total_sums(): sums = jnp.sum(lax.all_to_all(sent, 'row', 0, 0), axis=0)  5.53 us
    all_to_all x1, starting transfers between devices, total_sums(): sums = jnp.sum(lax.all_to_all(sent, 'row', 0, 0), axis=0)  3.25 us
  transfers between devices with their start and end apart: 7, of which 7 were waited for; matrix products, arithmetic and copies ran while one was open for 1% of the time, Pallas kernels for 0%

profile of v1, /device:TPU:0, one launch (start us, length us, event | category | flops | bytes accessed | tf_op | source)
XLA Modules:
  0.0 111.1 jit_solution(271862312865125374)
XLA Ops:
  0.6 0.7 fusion.41
  1.4 1.1 %fusion.40 = (f32[1,512]{1,0:T(1,128)S(1)}, f32[1,512]{1,0:T(1,128)S(1)}, f32[1,512]{1,0:T(1,128)S(1)}, f32[1,512]{1,0:T(1,128)S(1)}, f32[1,512]{1,0:T(1,128)S(1...) fusion(f32[36,512]{1,0:T(8,128)} %param.7), kind=kLoop, calls=%fused_computation.170 | loop fusion | bytes 77824 | tf_op jit(solution)/shard_map/slice | solution.py:22
  3.4 5.3 %all-to-all-start = ((f32[8,26,128]{2,1,0:T(8,128)}), f32[8,26,128]{2,1,0:T(8,128)S(1)}, u32[]{:S(2)}, u32[]{:S(2)}) async-start(f32[8,26,128]{2,1,0:T(8,128)} %broadcast_in_dim.16), calls=%async_computation | async-start | bytes 262144 | tf_op jit(solution)/shard_map/all_to_all | solution.py:139
  9.6 1.2 %copy.68 = f32[1,1,36,4096]{3,2,1,0:T(8,128)} copy(f32[1,1,36,4096]{3,1,2,0:T(1,128)S(1)} %copy-done) | data formatting | bytes 1179648
  10.9 3.3 %all-to-all-done = f32[8,26,128]{2,1,0:T(8,128)S(1)} async-done(((f32[8,26,128]{2,1,0:T(8,128)}), f32[8,26,128]{2,1,0:T(8,128)S(1)}, u32[]{:S(2)}, u32[]{:S(2)}) %all-to-all-start) | async-done | bytes 106528 | tf_op jit(solution)/shard_map/all_to_all | solution.py:139
  14.9 4.1 %tile_product.3 = f32[96,128]{1,0:T(8,128)} custom-call(s32[1,1]{1,0:T(1,128)S(6)} %copy.84.refs_0_, f32[192,128]{1,0:T(8,128)} %bitcast.147, s32[1,4096]{1,0:T(1,128)} %bitcast.162, s32[1,4096]{1,0:T(1,128)} %bitcast.165, f32[36,4096]{1,0:T(8,128)} %bitcast.129), custom_call_target="tpu_custom_call" | custom-call | tf_op jit(solution)/shard_map/tile_product/pallas_call | solution.py:107
  19.0 0.8 copy.34
  20.5 4.9 %all-to-all-start.1 = ((f32[4,26,128]{2,1,0:T(8,128)}), f32[4,26,128]{2,1,0:T(8,128)S(1)}, u32[]{:S(2)}, u32[]{:S(2)}) async-start(f32[4,26,128]{2,1,0:T(8,128)} %pad_maximum_fusion), calls=%async_computation.1 | async-start | bytes 131072 | tf_op jit(solution)/shard_map/all_to_all | solution.py:147
  25.4 5.7 %all-to-all-done.1 = f32[4,26,128]{2,1,0:T(8,128)S(1)} async-done(((f32[4,26,128]{2,1,0:T(8,128)}), f32[4,26,128]{2,1,0:T(8,128)S(1)}, u32[]{:S(2)}, u32[]{:S(2)}) %all-to-all-start.1) | async-done | bytes 53280 | tf_op jit(solution)/shard_map/all_to_all | solution.py:147
  32.0 4.1 %all-to-all-start.2 = ((f32[8,26,128]{2,1,0:T(8,128)}), f32[8,26,128]{2,1,0:T(8,128)S(1)}, u32[]{:S(2)}, u32[]{:S(2)}) async-start(f32[8,26,128]{2,1,0:T(8,128)} %broadcast_in_dim.18), calls=%async_computation.2 | async-start | bytes 262144 | tf_op jit(solution)/shard_map/all_to_all | solution.py:139
  36.1 5.5 %all-to-all-done.2 = f32[8,26,128]{2,1,0:T(8,128)S(1)} async-done(((f32[8,26,128]{2,1,0:T(8,128)}), f32[8,26,128]{2,1,0:T(8,128)S(1)}, u32[]{:S(2)}, u32[]{:S(2)}) %all-to-all-start.2) | async-done | bytes 106528 | tf_op jit(solution)/shard_map/all_to_all | solution.py:139
  42.3 4.1 %tile_product.4 = f32[96,128]{1,0:T(8,128)} custom-call(s32[1,1]{1,0:T(1,128)S(6)} %copy.84.refs_0_, f32[192,128]{1,0:T(8,128)} %bitcast.148, s32[1,4096]{1,0:T(1,128)} %bitcast.163, s32[1,4096]{1,0:T(1,128)} %bitcast.166, f32[36,4096]{1,0:T(8,128)} %bitcast.130), custom_call_target="tpu_custom_call" | custom-call | tf_op jit(solution)/shard_map/tile_product/pallas_call | solution.py:107
  46.4 0.8 copy.37
  47.9 3.3 %all-to-all-start.3 = ((f32[4,26,128]{2,1,0:T(8,128)}), f32[4,26,128]{2,1,0:T(8,128)S(1)}, u32[]{:S(2)}, u32[]{:S(2)}) async-start(f32[4,26,128]{2,1,0:T(8,128)} %pad_maximum_fusion.1), calls=%async_computation.3 | async-start | bytes 131072 | tf_op jit(solution)/shard_map/all_to_all | solution.py:147
  51.2 5.7 %all-to-all-done.3 = f32[4,26,128]{2,1,0:T(8,128)S(1)} async-done(((f32[4,26,128]{2,1,0:T(8,128)}), f32[4,26,128]{2,1,0:T(8,128)S(1)}, u32[]{:S(2)}, u32[]{:S(2)}) %all-to-all-start.3) | async-done | bytes 53280 | tf_op jit(solution)/shard_map/all_to_all | solution.py:147
  59.8 3.4 %all-to-all-start.4 = ((f32[8,26,128]{2,1,0:T(8,128)}), f32[8,26,128]{2,1,0:T(8,128)S(1)}, u32[]{:S(2)}, u32[]{:S(2)}) async-start(f32[8,26,128]{2,1,0:T(8,128)} %broadcast_in_dim.20), calls=%async_computation.4 | async-start | bytes 262144 | tf_op jit(solution)/shard_map/all_to_all | solution.py:139
  63.2 5.4 %all-to-all-done.4 = f32[8,26,128]{2,1,0:T(8,128)S(1)} async-done(((f32[8,26,128]{2,1,0:T(8,128)}), f32[8,26,128]{2,1,0:T(8,128)S(1)}, u32[]{:S(2)}, u32[]{:S(2)}) %all-to-all-start.4) | async-done | bytes 106528 | tf_op jit(solution)/shard_map/all_to_all | solution.py:139
  69.3 4.1 %tile_product.5 = f32[96,128]{1,0:T(8,128)} custom-call(s32[1,1]{1,0:T(1,128)S(6)} %copy.84.refs_0_, f32[192,128]{1,0:T(8,128)} %bitcast.146, s32[1,4096]{1,0:T(1,128)} %bitcast.164, s32[1,4096]{1,0:T(1,128)} %bitcast.167, f32[36,4096]{1,0:T(8,128)} %bitcast.131), custom_call_target="tpu_custom_call" | custom-call | tf_op jit(solution)/shard_map/tile_product/pallas_call | solution.py:107
  73.4 0.8 copy.40
  74.9 3.3 %all-to-all-start.5 = ((f32[4,26,128]{2,1,0:T(8,128)}), f32[4,26,128]{2,1,0:T(8,128)S(1)}, u32[]{:S(2)}, u32[]{:S(2)}) async-start(f32[4,26,128]{2,1,0:T(8,128)} %pad_maximum_fusion.2), calls=%async_computation.5 | async-start | bytes 131072 | tf_op jit(solution)/shard_map/all_to_all | solution.py:147
  78.2 5.7 %all-to-all-done.5 = f32[4,26,128]{2,1,0:T(8,128)S(1)} async-done(((f32[4,26,128]{2,1,0:T(8,128)}), f32[4,26,128]{2,1,0:T(8,128)S(1)}, u32[]{:S(2)}, u32[]{:S(2)}) %all-to-all-start.5) | async-done | bytes 53280 | tf_op jit(solution)/shard_map/all_to_all | solution.py:147
  89.2 7.3 %all_to_all.40 = f32[8,2,128]{2,1,0:T(2,128)S(1)} all-to-all(f32[8,2,128]{2,1,0:T(2,128)S(1)} %broadcast_in_dim.22), channel_id=1, replica_groups=mesh['row'=4,'col'=8] {'col'}, dimensions={0} | all-to-all | bytes 16384 | tf_op jit(solution)/shard_map/all_to_all | solution.py:155
  97.1 3.2 %all-to-all-start.7 = ((f32[4,2,128]{2,1,0:T(2,128)}), f32[4,2,128]{2,1,0:T(2,128)S(1)}, u32[]{:S(2)}, u32[]{:S(2)}) async-start(f32[4,2,128]{2,1,0:T(2,128)} %broadcast_in_dim.23), calls=%async_computation.7 | async-start | bytes 8192 | tf_op jit(solution)/shard_map/all_to_all | solution.py:157
  100.4 5.5 %all-to-all-done.7 = f32[4,2,128]{2,1,0:T(2,128)S(1)} async-done(((f32[4,2,128]{2,1,0:T(2,128)}), f32[4,2,128]{2,1,0:T(2,128)S(1)}, u32[]{:S(2)}, u32[]{:S(2)}) %all-to-all-start.7) | async-done | bytes 4128 | tf_op jit(solution)/shard_map/all_to_all | solution.py:157
  (90 shorter events, 10.6 us)
Async XLA Ops:
  0.6 1.9 %copy-start.1 = (f32[6,512]{1,0:T(8,128)S(1)}, f32[6,512]{1,0:T(8,128)}, u32[]{:S(2)}) copy-start(f32[6,512]{1,0:T(8,128)} %param.6) | copy-start | bytes 36868
  1.4 8.2 %copy-start = (f32[1,1,36,4096]{3,1,2,0:T(1,128)S(1)}, f32[1,1,36,4096]{3,1,2,0:T(1,128)}, u32[]{:S(2)}) copy-start(f32[1,1,36,4096]{3,1,2,0:T(1,128)} %param.8) | copy-start | bytes 1769476
  3.4 5.3 %copy-start.2 = (f32[36,512]{1,0:T(8,128)S(1)}, f32[36,512]{1,0:T(8,128)}, u32[]{:S(2)}) copy-start(f32[36,512]{1,0:T(8,128)} %param.7) | copy-start | bytes 221188
  3.4 10.8 %all-to-all-start = ((f32[8,26,128]{2,1,0:T(8,128)}), f32[8,26,128]{2,1,0:T(8,128)S(1)}, u32[]{:S(2)}, u32[]{:S(2)}) async-start(f32[8,26,128]{2,1,0:T(8,128)} %broadcast_in_dim.16), calls=%async_computation | async-start | bytes 262144 | tf_op jit(solution)/shard_map/all_to_all | solution.py:139
  20.5 10.6 %all-to-all-start.1 = ((f32[4,26,128]{2,1,0:T(8,128)}), f32[4,26,128]{2,1,0:T(8,128)S(1)}, u32[]{:S(2)}, u32[]{:S(2)}) async-start(f32[4,26,128]{2,1,0:T(8,128)} %pad_maximum_fusion), calls=%async_computation.1 | async-start | bytes 131072 | tf_op jit(solution)/shard_map/all_to_all | solution.py:147
  32.0 9.6 %all-to-all-start.2 = ((f32[8,26,128]{2,1,0:T(8,128)}), f32[8,26,128]{2,1,0:T(8,128)S(1)}, u32[]{:S(2)}, u32[]{:S(2)}) async-start(f32[8,26,128]{2,1,0:T(8,128)} %broadcast_in_dim.18), calls=%async_computation.2 | async-start | bytes 262144 | tf_op jit(solution)/shard_map/all_to_all | solution.py:139
  47.9 9.0 %all-to-all-start.3 = ((f32[4,26,128]{2,1,0:T(8,128)}), f32[4,26,128]{2,1,0:T(8,128)S(1)}, u32[]{:S(2)}, u32[]{:S(2)}) async-start(f32[4,26,128]{2,1,0:T(8,128)} %pad_maximum_fusion.1), calls=%async_computation.3 | async-start | bytes 131072 | tf_op jit(solution)/shard_map/all_to_all | solution.py:147
  59.8 8.8 %all-to-all-start.4 = ((f32[8,26,128]{2,1,0:T(8,128)}), f32[8,26,128]{2,1,0:T(8,128)S(1)}, u32[]{:S(2)}, u32[]{:S(2)}) async-start(f32[8,26,128]{2,1,0:T(8,128)} %broadcast_in_dim.20), calls=%async_computation.4 | async-start | bytes 262144 | tf_op jit(solution)/shard_map/all_to_all | solution.py:139
  74.9 9.0 %all-to-all-start.5 = ((f32[4,26,128]{2,1,0:T(8,128)}), f32[4,26,128]{2,1,0:T(8,128)S(1)}, u32[]{:S(2)}, u32[]{:S(2)}) async-start(f32[4,26,128]{2,1,0:T(8,128)} %pad_maximum_fusion.2), calls=%async_computation.5 | async-start | bytes 131072 | tf_op jit(solution)/shard_map/all_to_all | solution.py:147
  97.1 8.8 %all-to-all-start.7 = ((f32[4,2,128]{2,1,0:T(2,128)}), f32[4,2,128]{2,1,0:T(2,128)S(1)}, u32[]{:S(2)}, u32[]{:S(2)}) async-start(f32[4,2,128]{2,1,0:T(2,128)} %broadcast_in_dim.23), calls=%async_computation.7 | async-start | bytes 8192 | tf_op jit(solution)/shard_map/all_to_all | solution.py:157

commit v2 on v1

v2 whole, which is shorter than its diff:
```python
import math

import jax
import jax.numpy as jnp
from jax import lax
from jax.experimental import pallas as pl
from jax.experimental.pallas import tpu as pltpu
from jax.sharding import PartitionSpec as P

ITERS = 3
LANES = 128
SUBS = 8


def factor_blocks(blocks):
    lower_part = {}
    reciprocals = []
    for j in range(6):
        pivot_value = blocks[7 * j]
        for k in range(j):
            pivot_value = pivot_value - lower_part[j, k] * lower_part[j, k]
        reciprocal = 1.0 / jnp.sqrt(pivot_value)
        reciprocals.append(reciprocal)
        for i in range(j + 1, 6):
            entry_value = blocks[6 * i + j]
            for k in range(j):
                entry_value = entry_value - lower_part[i, k] * lower_part[j, k]
            lower_part[i, j] = entry_value * reciprocal
    return (lower_part, reciprocals)


def apply_inverse(lower_part, reciprocals, vector):
    forward = []
    for i in range(6):
        running = vector[i]
        for k in range(i):
            running = running - lower_part[i, k] * forward[k]
        forward.append(running * reciprocals[i])
    backward = [None] * 6
    for i in range(5, -1, -1):
        running = forward[i]
        for k in range(i + 1, 6):
            running = running - lower_part[k, i] * backward[k]
        backward[i] = running * reciprocals[i]
    return backward


def split_three(value):
    high = value.astype(jnp.bfloat16)
    rest = value - high.astype(jnp.float32)
    middle = rest.astype(jnp.bfloat16)
    low = (rest - middle.astype(jnp.float32)).astype(jnp.bfloat16)
    return high, middle, low


def exact_dot(left, onehot, dims):
    parts = [
        lax.dot_general(piece, onehot, (dims, ((), ())), preferred_element_type=jnp.float32)
        for piece in split_three(left)
    ]
    return parts[2] + parts[1] + parts[0]


def tile_kernel(count_ref, got_ref, cols_ref, rows_ref, blocks_ref, out_ref, *, chunk):
    n_col, high = got_ref.shape[:2]
    n_row = out_ref.shape[0]
    high_in = n_col * high
    high_out = n_row * high
    slots = cols_ref.shape[1]
    live = count_ref[0, 0]
    comp = lax.broadcasted_iota(jnp.int32, (SUBS, LANES), 0)
    sums = jnp.where(comp >= 6, sum(got_ref[c, 0] for c in range(n_col)), 0.0)
    blank = jnp.zeros((SUBS, LANES), jnp.float32)
    for r in range(n_row):
        for h in range(high):
            out_ref[r, h] = sums if h == 0 else blank

    def one_chunk(start):
        table = got_ref[...].reshape(high_in * SUBS, LANES)
        cols = cols_ref[:, pl.ds(start, chunk)]
        rows = rows_ref[:, pl.ds(start, chunk)]
        lane_ids = lax.broadcasted_iota(jnp.int32, (LANES, chunk), 0)
        low_in = jnp.where(lane_ids == cols % LANES, 1.0, 0.0).astype(jnp.bfloat16)
        spread = exact_dot(table, low_in, ((1,), (0,)))
        cols_high = jnp.broadcast_to(cols // LANES, (SUBS, chunk))
        picked = jnp.zeros((SUBS, chunk), jnp.float32)
        for t in range(high_in):
            picked = jnp.where(cols_high == t, spread[SUBS * t : SUBS * (t + 1)], picked)
        is_live = lax.broadcasted_iota(jnp.int32, (1, chunk), 1) + start < live
        terms = []
        for a in range(6):
            entries = blocks_ref[6 * a : 6 * a + 6, pl.ds(start, chunk)]
            term = jnp.sum(entries * picked[:6], axis=0, keepdims=True)
            terms.append(jnp.where(is_live, term, 0.0))
        terms.append(jnp.zeros((SUBS - 6, chunk), jnp.float32))
        terms = jnp.concatenate(terms, axis=0)
        rows_high = jnp.broadcast_to(rows // LANES, (SUBS, chunk))
        placed = jnp.concatenate(
            [jnp.where(rows_high == t, terms, 0.0) for t in range(high_out)], axis=0
        )
        low_out = jnp.where(lane_ids == rows % LANES, 1.0, 0.0).astype(jnp.bfloat16)
        added = exact_dot(placed, low_out, ((1,), (1,)))
        out_ref[...] += added.reshape(out_ref.shape)

    for turn in range(slots // chunk):
        @pl.when(turn * chunk < live)
        def _():
            one_chunk(turn * chunk)


def tile_product(count, got, cols, rows, blocks, n_row):
    chunk = math.gcd(512, cols.shape[1])
    vmem = pl.BlockSpec(memory_space=pltpu.VMEM)
    return pl.pallas_call(
        lambda *refs: tile_kernel(*refs, chunk=chunk),
        out_shape=jax.ShapeDtypeStruct((n_row,) + got.shape[1:], jnp.float32),
        in_specs=[pl.BlockSpec(memory_space=pltpu.SMEM), vmem, vmem, vmem, vmem],
        out_specs=vmem,
        name="tile_product",
    )(count, got, cols, rows, blocks)


def stage(body, inputs, out_shapes, name):
    vmem = pl.BlockSpec(memory_space=pltpu.VMEM)
    return pl.pallas_call(
        lambda *refs: body(refs[: len(inputs)], refs[len(inputs) :]),
        out_shape=[jax.ShapeDtypeStruct(s, jnp.float32) for s in out_shapes],
        in_specs=[vmem] * len(inputs),
        out_specs=[vmem] * len(out_shapes),
        name=name,
    )(*inputs)


PAIRS = [(i, j) for j in range(6) for i in range(j + 1, 6)]


def read(ref):
    return [ref[i] for i in range(ref.shape[0])]


def write(ref, values):
    for i, value in enumerate(values):
        ref[i] = value


def read_factor(ref):
    values = read(ref)
    return dict(zip(PAIRS, values[6:])), values[:6]


def axpy(left, scale, right):
    return [a + scale * b for a, b in zip(left, right)]


def lane_sums(left, right):
    total = left[0] * right[0]
    for a, b in zip(left[1:], right[1:]):
        total = total + a * b
    return jnp.sum(total, axis=0, keepdims=True)


def send(ref, vector, sums):
    copies, high = ref.shape[:2]
    blank = jnp.zeros((1, LANES), jnp.float32)
    for h in range(high):
        tail = sums if h == 0 else [blank, blank]
        tile = jnp.concatenate([v[h : h + 1] for v in vector] + tail, axis=0)
        for c in range(copies):
            ref[c, h] = tile


def receive(back_ref, diag_ref, vector):
    n_row, high = back_ref.shape[:2]
    tiles = []
    for h in range(high):
        tile = back_ref[0, h]
        for r in range(1, n_row):
            tile = tile + back_ref[r, h]
        tiles.append(tile)
    image = []
    for a in range(6):
        own = diag_ref[6 * a] * vector[0]
        for b in range(1, 6):
            own = own + diag_ref[6 * a + b] * vector[b]
        image.append(jnp.concatenate([t[a : a + 1] for t in tiles], axis=0) + own)
    rho = jnp.sum(tiles[0][6:7], axis=1, keepdims=True)
    curv = jnp.sum(tiles[0][7:8], axis=1, keepdims=True)
    return image, rho, curv


def on_device(minus_gradient, diag_blocks, hess_blocks, block_rows, block_cols, block_counts):
    pose_dev = minus_gradient.shape[1]
    high = pose_dev // LANES
    n_row = lax.axis_size("row")
    n_col = lax.axis_size("col")
    diag = diag_blocks.reshape(36, high, LANES)
    blocks = hess_blocks.reshape(36, -1)
    rows = block_rows.reshape(1, -1)
    cols = block_cols.reshape(1, -1)
    start = minus_gradient.reshape(6, high, LANES)
    vec = (6, high, LANES)
    sent_shape = (n_col, high, SUBS, LANES)
    last_shape = (n_row * n_col, 2, LANES)
    one = (1, 1)

    def exchange(sent):
        got = lax.all_to_all(sent, "col", 0, 0)
        partial = tile_product(block_counts, got, cols, rows, blocks, n_row)
        return lax.all_to_all(partial, "row", 0, 0)

    def begin(ins, outs):
        residual_ref, diag_ref = ins
        sent_ref, factor_ref, precond_ref = outs
        lower, recips = factor_blocks(diag_ref)
        write(factor_ref, recips + [lower[p] for p in PAIRS])
        precond = apply_inverse(lower, recips, read(residual_ref))
        write(precond_ref, precond)
        blank = jnp.zeros((1, LANES), jnp.float32)
        send(sent_ref, precond, [blank, blank])

    sent, factor, precond = stage(begin, [start, diag], [sent_shape, (21,) + vec[1:], vec], "begin")
    back = exchange(sent)

    def first(ins, outs):
        back_ref, diag_ref, factor_ref, residual_ref, precond_ref = ins
        sent_ref, image_ref, image_pre_ref = outs
        residual, precond = read(residual_ref), read(precond_ref)
        image, _, _ = receive(back_ref, diag_ref, precond)
        image_pre = apply_inverse(*read_factor(factor_ref), image)
        write(image_ref, image)
        write(image_pre_ref, image_pre)
        send(sent_ref, image_pre, [lane_sums(residual, precond), lane_sums(image, precond)])

    sent, image, image_pre = stage(
        first, [back, diag, factor, start, precond], [sent_shape, vec, vec], "first"
    )

    state = [start, precond, image, image_pre]
    for k in range(ITERS - 1):
        final_sums = k + 2 == ITERS
        back = exchange(sent)

        def middle(ins, outs, k=k, final_sums=final_sums):
            back_ref, diag_ref, factor_ref = ins[:3]
            residual, precond, image, image_pre = [read(r) for r in ins[3:7]]
            image_next, rho, curv = receive(back_ref, diag_ref, image_pre)
            if k == 0:
                step = rho / curv
                direction, along, along_pre, along_next = precond, image, image_pre, image_next
                update = [step * d for d in direction]
            else:
                update, direction, along, along_pre, along_next = [read(r) for r in ins[7:12]]
                rho_before, step_before = ins[12][...], ins[13][...]
                ratio = rho / rho_before
                step = rho / (curv - ratio * rho / step_before)
                direction = axpy(precond, ratio, direction)
                along = axpy(image, ratio, along)
                along_pre = axpy(image_pre, ratio, along_pre)
                along_next = axpy(image_next, ratio, along_next)
                update = axpy(update, step, direction)
            residual = axpy(residual, -step, along)
            precond = axpy(precond, -step, along_pre)
            image = axpy(image, -step, along_next)
            sums = [lane_sums(residual, precond), lane_sums(image, precond)]
            image_pre = image
            if final_sums:
                both = jnp.concatenate(sums, axis=0)
                for d in range(outs[0].shape[0]):
                    outs[0][d] = both
            else:
                image_pre = apply_inverse(*read_factor(factor_ref), image)
                send(outs[0], image_pre, sums)
            values = [residual, precond, image, image_pre, update, direction, along, along_pre, along_next]
            for ref, value in zip(outs[1:10], values):
                write(ref, value)
            outs[10][...] = rho
            outs[11][...] = step

        sent, *state = stage(
            middle,
            [back, diag, factor] + state,
            [last_shape if final_sums else sent_shape] + [vec] * 9 + [one] * 2,
            "middle",
        )

    residual, precond, image, _, update, direction, along, _, _, rho, step = state
    totals = lax.all_to_all(sent, ("row", "col"), 0, 0)

    def end(ins, outs):
        both = ins[0][0]
        for d in range(1, ins[0].shape[0]):
            both = both + ins[0][d]
        rho = jnp.sum(both[0:1], axis=1, keepdims=True)
        curv = jnp.sum(both[1:2], axis=1, keepdims=True)
        residual, precond, image, update, direction, along = [read(r) for r in ins[1:7]]
        ratio = rho / ins[7][...]
        step = rho / (curv - ratio * rho / ins[8][...])
        write(outs[0], axpy(update, step, axpy(precond, ratio, direction)))
        write(outs[1], axpy(residual, -step, axpy(image, ratio, along)))

    update, residual = stage(
        end, [totals, residual, precond, image, update, direction, along, rho, step], [vec, vec], "end"
    )
    return (update.reshape(6, pose_dev), residual.reshape(6, pose_dev))


def solution(mesh):
    vectors = P(None, ("row", "col"))
    return jax.shard_map(
        on_device,
        mesh=mesh,
        in_specs=(
            vectors,
            vectors,
            P("row", "col", None, None),
            P("row", "col", None),
            P("row", "col", None),
            P("row", "col"),
        ),
        out_specs=(vectors, vectors),
        check_vma=False,
    )
```

time: 113 us -> 104 us (0.920)
  blocking collectives: 7.35 us -> 58.5 us
  waiting for transfers between devices: 36.8 us -> 2.59 us
  starting transfers between devices: 27.5 us -> 5.2 us
  Pallas kernels: 12.3 us -> 28.1 us
  between operations: 11.1 us -> 1.3 us
  local copies, waits for them, and re-layouts: 12.2 us -> 7.13 us
  other arithmetic: 3.81 us -> 0 us
    all_to_all x1 -> x6, blocking collectives: 7.35 us -> 58.5 us  [the longest x3 29.1 us: exchange(): return lax.all_to_all(partial, 'row', 0, 0)]
    all_to_all x7 -> x1, waiting for transfers between devices: 36.8 us -> 2.59 us  [exchange(): got = lax.all_to_all(sent, 'col', 0, 0)]
    all_to_all x7 -> x1, starting transfers between devices: 27.5 us -> 5.2 us  [exchange(): got = lax.all_to_all(sent, 'col', 0, 0)]
    pallas_call x0 -> x5, Pallas kernels: none -> 11 us  [stage(): pl.pallas_call(lambda *refs: body(refs[:len(inputs)], refs[len(inputs):])...]
    pallas_call x3, Pallas kernels: 12.3 us -> 17.2 us  [tile_product(): pl.pallas_call(lambda *refs: tile_kernel(*refs, chunk=chunk), out_shape=j...]
    slice x9 -> x0, local copies, waits for them, and re-layouts: 3.75 us -> none  [the longest x3 1.84 us: on_device(): rho, curv = (totals[0], totals[1])]
    broadcast_in_dim x8 -> x0, local copies, waits for them, and re-layouts: 2.56 us -> none  [the longest x3 1.94 us: hessian(): sent = jnp.broadcast_to(mine[None], (n_col,) + mine.shape)]
    transpose x3 -> x0, local copies, waits for them, and re-layouts: 1.99 us -> none  [hessian(): table = jnp.transpose(table, (1, 0, 2, 3)).reshape(6 * n_col * high, LANES)]
  transfers between devices with their start and end apart: 7 -> 1, of which waited for: 7 -> 1; matrix products, arithmetic and copies ran while one was open for 1% -> 2% of each run, Pallas kernels for 0% -> 0%
where the time goes in v2:
time: 104 us; the launch traced here: 103 us
  blocking collectives  58.5 us (56%)
  Pallas kernels  28.1 us (27%)
  local copies, waits for them, and re-layouts  7.13 us (7%)
  starting transfers between devices  5.2 us (5%)
  waiting for transfers between devices  2.59 us (2%)
  between operations  1.3 us (1%)
    all_to_all x3, blocking collectives, exchange(): return lax.all_to_all(partial, 'row', 0, 0)  29.1 us
    all_to_all x2, blocking collectives, exchange(): got = lax.all_to_all(sent, 'col', 0, 0)  19 us
    pallas_call x3, Pallas kernels, tile_product(): pl.pallas_call(lambda *refs: tile_kernel(*refs, chunk=chunk), out_shape=j...  17.2 us
    pallas_call x5, Pallas kernels, stage(): pl.pallas_call(lambda *refs: body(refs[:len(inputs)], refs[len(inputs):])...  11 us
    all_to_all x1, blocking collectives, on_device(): totals = lax.all_to_all(sent, ('row', 'col'), 0, 0)  10.5 us
    all_to_all x1, starting transfers between devices, exchange(): got = lax.all_to_all(sent, 'col', 0, 0)  5.2 us
    unnamed x3, local copies, waits for them, and re-layouts  2.92 us
    all_to_all x1, waiting for transfers between devices, exchange(): got = lax.all_to_all(sent, 'col', 0, 0)  2.59 us
  transfers between devices with their start and end apart: 1, of which 1 were waited for; matrix products, arithmetic and copies ran while one was open for 2% of the time, Pallas kernels for 0%

profile of v2, /device:TPU:0, one launch (start us, length us, event | category | flops | bytes accessed | tf_op | source)
XLA Modules:
  0.0 102.9 jit_solution(7494075226918122798)
XLA Ops:
  0.6 1.3 %reshape.25.refs_0_.refs_3_ = f32[6,4,128]{2,1,0:T(4,128)} reshape(f32[6,512]{1,0:T(8,128)} %param.6) | data formatting | bytes 24576 | tf_op jit(solution)/shard_map/reshape | solution.py:200
  2.0 1.5 %reshape.26.refs_1_ = f32[36,4,128]{2,1,0:T(4,128)} reshape(f32[36,512]{1,0:T(8,128)} %param.7) | data formatting | bytes 147456 | tf_op jit(solution)/shard_map/reshape | solution.py:196
  3.5 1.7 %begin.1 = (f32[8,4,8,128]{3,2,1,0:T(8,128)}, f32[21,4,128]{2,1,0:T(4,128)}, f32[6,4,128]{2,1,0:T(4,128)}) custom-call(f32[6,4,128]{2,1,0:T(4,128)} %reshape.25.refs_0_.refs_3_, f32[36,4,128]{2,1,0:T(4,128)} %reshape.26.refs_1_), custom_call_target="tpu_custom_call" | custom-call | tf_op jit(solution)/shard_map/begin/pallas_call | solution.py:125
  5.2 5.2 %all-to-all-start = ((f32[8,4,8,128]{3,2,1,0:T(8,128)}), f32[8,4,8,128]{3,2,1,0:T(8,128)S(1)}, u32[]{:S(2)}, u32[]{:S(2)}) async-start(f32[8,4,8,128]{3,2,1,0:T(8,128)} %get-tuple-element.31), calls=%async_computation | async-start | bytes 262144 | tf_op jit(solution)/shard_map/all_to_all | solution.py:207
  11.1 2.3 %copy.14 = f32[1,1,36,4096]{3,2,1,0:T(8,128)} copy(f32[1,1,36,4096]{3,1,2,0:T(1,128)} %param.8) | data formatting | bytes 1179648
  13.3 2.6 %all-to-all-done.refs_1_ = f32[8,4,8,128]{3,2,1,0:T(8,128)S(1)} async-done(((f32[8,4,8,128]{3,2,1,0:T(8,128)}), f32[8,4,8,128]{3,2,1,0:T(8,128)S(1)}, u32[]{:S(2)}, u32[]{:S(2)}) %all-to-all-start) | async-done | bytes 131104 | tf_op jit(solution)/shard_map/all_to_all | solution.py:207
  15.9 0.0 copy-start
  15.9 0.7 copy-done
  16.6 5.7 %tile_product.3 = f32[4,4,8,128]{3,2,1,0:T(8,128)} custom-call(s32[1,1]{1,0:T(1,128)S(6)} %copy.15.refs_0_, f32[8,4,8,128]{3,2,1,0:T(8,128)} %copy-done, s32[1,4096]{1,0:T(1,128)} %bitcast.14, s32[1,4096]{1,0:T(1,128)} %bitcast.17, f32[36,4096]{1,0:T(8,128)} %bitcast.11), custom_call_target="tpu_custom_call" | custom-call | tf_op jit(solution)/shard_map/tile_product/pallas_call | solution.py:114
  22.3 9.7 %all_to_all.35.refs_0_ = f32[4,4,8,128]{3,2,1,0:T(8,128)} all-to-all(f32[4,4,8,128]{3,2,1,0:T(8,128)} %tile_product.3), channel_id=1, replica_groups=mesh['row'=4,'col'=8] {'row'}, dimensions={0} | all-to-all | bytes 131072 | tf_op jit(solution)/shard_map/all_to_all | solution.py:209
  32.0 1.6 %first.1 = (f32[8,4,8,128]{3,2,1,0:T(8,128)}, f32[6,4,128]{2,1,0:T(4,128)}, f32[6,4,128]{2,1,0:T(4,128)}) custom-call(f32[4,4,8,128]{3,2,1,0:T(8,128)} %all_to_all.35.refs_0_, f32[36,4,128]{2,1,0:T(4,128)} %reshape.26.refs_1_, f32[21,4,128]{2,1,0:T(4,128)} %get-tuple-element.32.refs_2_, f32[6,4,128]{2,1,0:T(4,128)} %reshape.25.refs_0_.refs_3_, ...), custom_call_target="tpu_custom_call" | custom-call | tf_op jit(solution)/shard_map/first/pallas_call | solution.py:125
  33.6 9.5 %all_to_all.36.refs_1_ = f32[8,4,8,128]{3,2,1,0:T(8,128)} all-to-all(f32[8,4,8,128]{3,2,1,0:T(8,128)} %get-tuple-element.34), channel_id=1, replica_groups=mesh['row'=4,'col'=8] {'col'}, dimensions={0} | all-to-all | bytes 262144 | tf_op jit(solution)/shard_map/all_to_all | solution.py:207
  43.1 5.7 %tile_product.4 = f32[4,4,8,128]{3,2,1,0:T(8,128)} custom-call(s32[1,1]{1,0:T(1,128)S(6)} %copy.15.refs_0_, f32[8,4,8,128]{3,2,1,0:T(8,128)} %all_to_all.36.refs_1_, s32[1,4096]{1,0:T(1,128)} %bitcast.15, s32[1,4096]{1,0:T(1,128)} %bitcast.18, f32[36,4096]{1,0:T(8,128)} %bitcast.12), custom_call_target="tpu_custom_call" | custom-call | tf_op jit(solution)/shard_map/tile_product/pallas_call | solution.py:114
  48.8 9.7 %all_to_all.37.refs_0_ = f32[4,4,8,128]{3,2,1,0:T(8,128)} all-to-all(f32[4,4,8,128]{3,2,1,0:T(8,128)} %tile_product.4), channel_id=1, replica_groups=mesh['row'=4,'col'=8] {'row'}, dimensions={0} | all-to-all | bytes 131072 | tf_op jit(solution)/shard_map/all_to_all | solution.py:209
  58.5 1.8 %middle.2 = (f32[8,4,8,128]{3,2,1,0:T(8,128)}, f32[6,4,128]{2,1,0:T(4,128)}, f32[6,4,128]{2,1,0:T(4,128)}, f32[6,4,128]{2,1,0:T(4,128)}, f32[6,4,128]{2,1,0:T(4,...) custom-call(f32[4,4,8,128]{3,2,1,0:T(8,128)} %all_to_all.37.refs_0_,, ...), custom_call_target="tpu_custom_call" | custom-call | tf_op jit(solution)/shard_map/middle/pallas_call | solution.py:125
  60.3 9.5 %all_to_all.38.refs_1_ = f32[8,4,8,128]{3,2,1,0:T(8,128)} all-to-all(f32[8,4,8,128]{3,2,1,0:T(8,128)} %get-tuple-element.37), channel_id=1, replica_groups=mesh['row'=4,'col'=8] {'col'}, dimensions={0} | all-to-all | bytes 262144 | tf_op jit(solution)/shard_map/all_to_all | solution.py:207
  69.8 5.7 %tile_product.5 = f32[4,4,8,128]{3,2,1,0:T(8,128)} custom-call(s32[1,1]{1,0:T(1,128)S(6)} %copy.15.refs_0_, f32[8,4,8,128]{3,2,1,0:T(8,128)} %all_to_all.38.refs_1_, s32[1,4096]{1,0:T(1,128)} %bitcast.16, s32[1,4096]{1,0:T(1,128)} %bitcast.19, f32[36,4096]{1,0:T(8,128)} %bitcast.13), custom_call_target="tpu_custom_call" | custom-call | tf_op jit(solution)/shard_map/tile_product/pallas_call | solution.py:114
  75.6 9.7 %all_to_all.39.refs_0_ = f32[4,4,8,128]{3,2,1,0:T(8,128)} all-to-all(f32[4,4,8,128]{3,2,1,0:T(8,128)} %tile_product.5), channel_id=1, replica_groups=mesh['row'=4,'col'=8] {'row'}, dimensions={0} | all-to-all | bytes 131072 | tf_op jit(solution)/shard_map/all_to_all | solution.py:209
  85.3 3.0 %middle.3 = (f32[32,2,128]{2,1,0:T(2,128)}, f32[6,4,128]{2,1,0:T(4,128)}, f32[6,4,128]{2,1,0:T(4,128)}, f32[6,4,128]{2,1,0:T(4,128)}, f32[6,4,128]{2,1,0:T(4,128...) custom-call(f32[4,4,8,128]{3,2,1,0:T(8,128)} %all_to_all.39.refs_0_,, ...), custom_call_target="tpu_custom_call" | custom-call | tf_op jit(solution)/shard_map/middle/pallas_call | solution.py:125
  88.3 10.5 %all_to_all.40.refs_0_ = f32[32,2,128]{2,1,0:T(2,128)} all-to-all(f32[32,2,128]{2,1,0:T(2,128)} %get-tuple-element.49), channel_id=1, replica_groups=mesh['row'=4,'col'=8] {'row','col'}, dimensions={0} | all-to-all | bytes 65536 | tf_op jit(solution)/shard_map/all_to_all | solution.py:287
  98.7 2.8 %end.1 = (f32[6,4,128]{2,1,0:T(4,128)}, f32[6,4,128]{2,1,0:T(4,128)}) custom-call(f32[32,2,128]{2,1,0:T(2,128)} %all_to_all.40.refs_0_, f32[6,4,128]{2,1,0:T(4,128)} %get-tuple-element.50.refs_1_, f32[6,4,128]{2,1,0:T(4,128)} %get-tuple-element.51.refs_2_, f32[6,4,128]{2,1,0:T(4,128)} %get-tuple-element.52.refs_3_, f32[6,4,128]{2,1,0:T(4,128)} %get-tuple-element.53.refs_4_, ...), custom_call_target="tpu_custom_call" | custom-call | tf_op jit(solution)/shard_map/end/pallas_call | solution.py:125
  101.6 1.3 %copy_bitcast_fusion.1 = (f32[6,512]{1,0:T(8,128)}, f32[6,512]{1,0:T(8,128)}) fusion(f32[1,6,4,128]{3,2,1,0:T(4,128)} %bitcast.21, f32[1,6,4,128]{3,2,1,0:T(4,128)} %bitcast.20), kind=kLoop, calls=%fused_computation.1 | loop fusion | bytes 49152 | tf_op jit(solution)/shard_map/reshape | solution.py:304
Async XLA Ops:
  5.2 10.7 %all-to-all-start = ((f32[8,4,8,128]{3,2,1,0:T(8,128)}), f32[8,4,8,128]{3,2,1,0:T(8,128)S(1)}, u32[]{:S(2)}, u32[]{:S(2)}) async-start(f32[8,4,8,128]{3,2,1,0:T(8,128)} %get-tuple-element.31), calls=%async_computation | async-start | bytes 262144 | tf_op jit(solution)/shard_map/all_to_all | solution.py:207
  15.9 0.7 copy-start
